TPU v7x, 256 devices: a whole 4x4x8 slice. The times are simulated.
256 devices in a mesh: ops: 64 (over x, z, core), sec: 4 (over y).
Axes of the slice: x: 4, y: 4, z: 8, core: 2. Of those that a mesh axis runs over, the one named last changes fastest.
Arguments:
- operators: bfloat16 [128, 8, 768, 768], P('ops', 'sec'), may hold values from -6 to 6
- basis: bfloat16 [8, 768, 768], P('sec'), may hold values from -0.21875 to 0.21875
- shift: int32 [128], replicated, may hold values from -1 to 1
- dest: int32 [128], replicated, may hold values from 0 to 127, each once
- sector_sizes: int32 [8], replicated, may hold values from 384 to 768
Outputs:
- renormalized: bfloat16 [128, 8, 768, 768], P('ops', 'sec')
Inputs may be any that keep to these rules, and one draw needn't show every extreme that they name: `shift`: each pair's offset is -1, 0 or 1. dest names every index of 0 to 127 once.
All inputs are finite; a program needn't handle non-finite values.
Results may differ from a plain program's by a relative error of at most 0.0049.
Values may be sent and summed in bfloat16 or wider, within the bound.
A program may use at most 128 MiB of HBM per device.

v0:
```python
import jax
import jax.numpy as jnp
from jax import lax
from jax.sharding import PartitionSpec as P


def with_halo(block, sides, width):
    for axis, dim in sides:
        count = lax.axis_size(axis)
        forward = [(i, i + 1) for i in range(count - 1)]
        forward.append((count - 1, 0))
        backward = [(target, source) for source, target in forward]
        low = lax.ppermute(
            lax.slice_in_dim(block, block.shape[dim] - width, None, axis=dim), axis, forward
        )
        high = lax.ppermute(lax.slice_in_dim(block, 0, width, axis=dim), axis, backward)
        block = jnp.concatenate([low, block, high], axis=dim)
    return block


def body(operators, basis, shift, dest, sector_sizes):
    pair_dev = operators.shape[0]
    sector_dev = operators.shape[1]
    width = operators.shape[3]
    ops_count = lax.axis_size("ops")
    total_sectors = sector_dev * lax.axis_size("sec")
    sector_pos = lax.axis_index("sec")
    ops_pos = lax.axis_index("ops")
    nearby = with_halo(basis, (("sec", 0),), 1)
    near_ids = (
        sector_pos * sector_dev - 1 + jnp.arange(sector_dev + 2, dtype=jnp.int32)
    ) % total_sectors
    own_local = jnp.arange(sector_dev, dtype=jnp.int32) + 1
    columns = jnp.arange(width, dtype=jnp.int32)
    near_sizes = jnp.take(sector_sizes, near_ids)
    kept = columns[None, :] < near_sizes[:, None]
    kept_near = jnp.where(kept[:, None, :], nearby, jnp.zeros_like(nearby))
    own_basis = jnp.take(kept_near, own_local, axis=0)
    source = jnp.argsort(dest, stable=True)
    mine = lax.dynamic_slice_in_dim(source, ops_pos * pair_dev, pair_dev)
    offsets = jnp.take(shift, mine)
    strip = width // ops_count
    split = operators.reshape(pair_dev, sector_dev, ops_count, strip, width)
    spread = lax.all_to_all(split, "ops", split_axis=2, concat_axis=0, tiled=True)
    ordered = jnp.take(spread, source, axis=0)
    returned = lax.all_to_all(ordered, "ops", split_axis=0, concat_axis=2, tiled=True)
    blocks = returned.reshape(pair_dev, sector_dev, width, width)
    target_local = own_local[None, :] + offsets[:, None]
    half = jnp.einsum(
        "psab,sbc->psac", blocks, own_basis, preferred_element_type=jnp.float32
    ).astype(jnp.bfloat16)
    targets = jnp.take(kept_near, target_local.reshape(-1), axis=0)
    targets = targets.reshape(blocks.shape[0], sector_dev, width, width)
    return jnp.einsum("psba,psbc->psac", targets, half, preferred_element_type=jnp.float32).astype(
        jnp.bfloat16
    )


def solution(mesh):
    return jax.shard_map(
        body,
        mesh=mesh,
        in_specs=(P("ops", "sec", None, None), P("sec", None, None), P(), P(), P()),
        out_specs=P("ops", "sec", None, None),
        check_vma=False,
    )
```

profile of v0, /device:TPU:1, one launch (start us, length us, event | category | flops | bytes accessed | tf_op | source)
XLA Modules:
  0.0 295.1 jit_solution(11162149202697768702)
XLA Ops:
  0.0 0.0 copy-start
  0.0 9.4 %copy.12 = bf16[2,2,768,768]{3,1,2,0:T(2,128)(2,1)} copy(bf16[2,2,768,768]{3,2,1,0:T(8,128)(2,1)} %param.5) | data formatting | bytes 9437184 | tf_op args[0]
  9.4 7.7 %copy.13 = bf16[2,2,64,12,768]{4,1,3,0,2:T(2,128)(2,1)} copy(bf16[2,2,64,12,768]{4,1,3,2,0:T(2,128)(2,1)} %bitcast.33) | data formatting | bytes 9437184 | tf_op jit(solution)/shard_map/reshape | solution.py:43
  17.1 0.0 copy-start.5
  17.1 13.3 %all-to-all-start = ((bf16[2,2,64,12,768]{4,1,3,0,2:T(2,128)(2,1)}), bf16[2,2,64,12,768]{4,1,3,0,2:T(2,128)(2,1)}, u32[]{:S(2)}, u32[]{:S(2)}) async-start(bf16[2,2,64,12,768]{4,1,3,0,2:T(2,128)(2,1)} %copy.13), calls=%async_computation | async-start | bytes 9437184 | tf_op jit(solution)/shard_map/all_to_all | solution.py:44
  30.4 0.0 copy-done.5
  30.5 2.5 sort.17
  33.0 0.0 copy-start.4
  33.0 104.5 %all-to-all-done = bf16[2,2,64,12,768]{4,1,3,0,2:T(2,128)(2,1)} async-done(((bf16[2,2,64,12,768]{4,1,3,0,2:T(2,128)(2,1)}), bf16[2,2,64,12,768]{4,1,3,0,2:T(2,128)(2,1)}, u32[]{:S(2)}, u32[]{:S(2)}) %all-to-all-start) | async-done | bytes 4718624 | tf_op jit(solution)/shard_map/all_to_all | solution.py:44
  137.5 15.6 %gather_fusion.4 = bf16[128,2,12,768]{3,1,2,0:T(2,128)(2,1)} fusion(bf16[128,2,12,768]{3,1,2,0:T(2,128)(2,1)} %bitcast.8, s32[1024]{0:T(1024)S(1)} %pad_clamp_fusion), kind=kCustom, calls=%fused_computation.4 | custom fusion | bytes 9437696 | tf_op jit(solution)/shard_map/jit(_take)/gather | solution.py:45
  153.1 8.8 %fusion.6 = bf16[128,2,1,12,768]{4,1,3,2,0:T(2,128)(2,1)} fusion(bf16[128,2,12,768]{3,1,2,0:T(2,128)(2,1)} %gather_fusion.4, pred[128]{0:T(512)(128)(4,1)S(1)} %compare_and_fusion), kind=kLoop, calls=%fused_computation.13 | loop fusion | flops 2359296 | bytes 9437312 | tf_op jit(solution)/shard_map/jit(_take)/select_n | solution.py:45
  161.9 0.0 copy-start.2
  161.9 6.1 %all-to-all-start.1 = ((bf16[128,2,1,12,768]{4,1,3,2,0:T(2,128)(2,1)}), bf16[128,2,1,12,768]{4,1,3,2,0:T(2,128)(2,1)}, u32[]{:S(2)}, u32[]{:S(2)}) async-start(bf16[128,2,1,12,768]{4,1,3,2,0:T(2,128)(2,1)} %fusion.6), calls=%async_computation.1 | async-start | bytes 9437184 | tf_op jit(solution)/shard_map/all_to_all | solution.py:46
  168.0 0.0 copy-done.2
  168.1 0.0 copy-start.1
  168.1 1.6 fusion.33
  169.6 1.3 collective-permute-start
  170.9 1.4 collective-permute-start.1
  172.4 0.0 copy-done.4
  172.4 0.1 compare_select_fusion.7
  172.5 0.0 copy-done.1
  172.5 1.2 gather_fusion
  173.6 0.7 and_select_fusion.3
  174.3 0.0 copy-start.3
  174.3 0.1 broadcast_add_fusion
  174.4 0.7 add.175
  175.1 0.0 copy-done
  175.1 1.2 gather_fusion.1
  176.3 0.5 compare_and_fusion.1
  176.8 0.7 fusion.30
  177.5 0.0 copy-done.3
  177.5 0.7 and_select_fusion.1
  178.2 1.3 compare_and_fusion.2
  179.4 0.1 iota_compare_fusion
  179.5 18.7 %collective-permute-done = bf16[1,768,768]{2,1,0:T(8,128)(2,1)S(1)} collective-permute-done((bf16[1,768,768]{2,1,0:T(8,128)(2,1)}, bf16[1,768,768]{2,1,0:T(8,128)(2,1)S(1)}, u32[]{:S(2)}, u32[]{:S(2)}) %collective-permute-start) | collective-permute-done | bytes 1179680 | tf_op jit(solution)/shard_map/ppermute | solution.py:13
  198.2 0.0 collective-permute-done.1
  198.2 3.7 %maximum_select_fusion = bf16[4,768,768]{2,1,0:T(8,128)(2,1)} fusion(bf16[1,768,768]{2,1,0:T(8,128)(2,1)} %collective-permute-done.1, bf16[2,768,768]{2,1,0:T(8,128)(2,1)S(1)} %copy-done.2, bf16[1,768,768]{2,1,0:T(8,128)(2,1)S(1)} %collective-permute-done, pred[4,768]{1,0:T(4,128)(4,1)S(1)} %iota_compare_fusion), kind=kLoop, calls=%fused_computation.6 | loop fusion | flops 7077888 | bytes 9440256 | tf_op jit(solution)/shard_map/jit(_where)/select_n | solution.py:37
  201.9 5.3 %gather_fusion.2 = bf16[4,768,768]{2,1,0:T(8,128)(2,1)} fusion(bf16[4,768,768]{2,1,0:T(8,128)(2,1)} %maximum_select_fusion, s32[1024]{0:T(1024)S(1)} %pad_clamp_fusion.2), kind=kCustom, calls=%fused_computation.2 | custom fusion | bytes 9437200 | tf_op jit(solution)/shard_map/jit(_take)/gather | solution.py:52
  207.2 6.6 %copy.11 = bf16[2,2,768,768]{2,3,1,0:T(8,128)(2,1)} copy(bf16[2,2,768,768]{3,2,1,0:T(8,128)(2,1)} %bitcast.32) | data formatting | bytes 9437184 | tf_op jit(solution)/shard_map/jit(_take)/gather | solution.py:52
  213.8 3.0 %gather_fusion.3 = bf16[2,768,768]{2,1,0:T(8,128)(2,1)S(1)} fusion(bf16[4,768,768]{2,1,0:T(8,128)(2,1)} %maximum_select_fusion, s32[1024]{0:T(1024)S(1)} %pad_clamp_fusion.1), kind=kCustom, calls=%fused_computation.3 | custom fusion | bytes 4718600 | tf_op jit(solution)/shard_map/jit(_take)/gather | solution.py:38
  216.9 58.3 %all-to-all-done.1 = bf16[128,2,1,12,768]{4,1,3,2,0:T(2,128)(2,1)} async-done(((bf16[128,2,1,12,768]{4,1,3,2,0:T(2,128)(2,1)}), bf16[128,2,1,12,768]{4,1,3,2,0:T(2,128)(2,1)}, u32[]{:S(2)}, u32[]{:S(2)}) %all-to-all-start.1) | async-done | bytes 4718624 | tf_op jit(solution)/shard_map/all_to_all | solution.py:46
  275.2 0.0 copy-start.6
  275.2 0.0 copy-start.7
  275.2 7.8 %copy.15 = bf16[64,2,2,1,12,768]{5,2,4,0,1,3:T(2,128)(2,1)} copy(bf16[64,2,2,1,12,768]{5,2,4,1,0,3:T(2,128)(2,1)} %bitcast.11) | data formatting | bytes 9437184 | tf_op jit(solution)/shard_map/all_to_all | solution.py:46
  282.9 0.0 copy-done.6
  282.9 0.0 copy-done.7
  282.9 12.2 %fusion.8 = bf16[2,2,768,768]{3,2,1,0:T(8,128)(2,1)} fusion(bf16[2,2,768,768]{2,3,1,0:T(8,128)(2,1)} %copy.11, pred[2,2]{1,0:T(4,128)(4,1)S(1)} %copy-done.6, bf16[2,2,768,768]{3,1,2,0:T(2,128)(2,1)} %bitcast.34, bf16[2,768,768]{2,1,0:T(8,128)(2,1)S(1)} %gather_fusion.3, pred[2]{0:T(512)(128)(4,1)S(1)} %copy-done.7), kind=kOutput, calls=%fused_computation.15 | convolution fusion | flops 7256014848 | bytes 16515078 | tf_op jit(solution)/shard_map/psba,psbc->psac/dot_general | solution.py:54
  (10 shorter events, 0.1 us)
Async XLA Ops:
  0.0 175.1 %copy-start = (s32[8]{0:T(128)S(1)}, s32[8]{0:T(128)}, u32[]{:S(2)}) copy-start(s32[8]{0:T(128)} %param.9) | copy-start | bytes 100
  17.1 13.3 %copy-start.5 = (s32[128]{0:T(128)S(1)}, s32[128]{0:T(128)}, u32[]{:S(2)}) copy-start(s32[128]{0:T(128)} %param.8) | copy-start | bytes 1540
  17.1 120.4 %all-to-all-start = ((bf16[2,2,64,12,768]{4,1,3,0,2:T(2,128)(2,1)}), bf16[2,2,64,12,768]{4,1,3,0,2:T(2,128)(2,1)}, u32[]{:S(2)}, u32[]{:S(2)}) async-start(bf16[2,2,64,12,768]{4,1,3,0,2:T(2,128)(2,1)} %copy.13), calls=%async_computation | async-start | bytes 9437184 | tf_op jit(solution)/shard_map/all_to_all | solution.py:44
  33.0 139.4 %copy-start.4 = (s32[128]{0:T(128)}, s32[128]{0:T(128)S(1)}, u32[]{:S(2)}) copy-start(s32[128]{0:T(128)S(1)} %get-tuple-element.6) | copy-start | bytes 1540
  161.9 6.1 %copy-start.2 = (bf16[2,768,768]{2,1,0:T(8,128)(2,1)S(1)}, bf16[2,768,768]{2,1,0:T(8,128)(2,1)}, u32[]{:S(2)}) copy-start(bf16[2,768,768]{2,1,0:T(8,128)(2,1)} %param.6) | copy-start | bytes 7077892
  161.9 113.3 %all-to-all-start.1 = ((bf16[128,2,1,12,768]{4,1,3,2,0:T(2,128)(2,1)}), bf16[128,2,1,12,768]{4,1,3,2,0:T(2,128)(2,1)}, u32[]{:S(2)}, u32[]{:S(2)}) async-start(bf16[128,2,1,12,768]{4,1,3,2,0:T(2,128)(2,1)} %fusion.6), calls=%async_computation.1 | async-start | bytes 9437184 | tf_op jit(solution)/shard_map/all_to_all | solution.py:46
  168.1 4.4 %copy-start.1 = (s32[128]{0:T(128)S(1)}, s32[128]{0:T(128)}, u32[]{:S(2)}) copy-start(s32[128]{0:T(128)} %param.7) | copy-start | bytes 1540
  169.6 28.6 %collective-permute-start = (bf16[1,768,768]{2,1,0:T(8,128)(2,1)}, bf16[1,768,768]{2,1,0:T(8,128)(2,1)S(1)}, u32[]{:S(2)}, u32[]{:S(2)}) collective-permute-start(bf16[1,768,768]{2,1,0:T(8,128)(2,1)} %get-tuple-element.7), channel_id=1, source_target_pairs={{0,1},{1,2},{2,3},{3,0},{4,5},{5,6},{6,7},{7,4},{8,9},{9,10},{10,1... | collective-permute-start | bytes 3538952 | tf_op jit(solution)/shard_map/ppermute | solution.py:13
  170.9 27.3 %collective-permute-start.1 = (bf16[1,768,768]{2,1,0:T(8,128)(2,1)}, bf16[1,768,768]{2,1,0:T(8,128)(2,1)}, u32[]{:S(2)}, u32[]{:S(2)}) collective-permute-start(bf16[1,768,768]{2,1,0:T(8,128)(2,1)} %get-tuple-element.8), channel_id=1, source_target_pairs={{1,0},{2,1},{3,2},{0,3},{5,4},{6,5},{7,6},{4,7},{9,8},{10,9},{11,1... | collective-permute-start | bytes 3538952 | tf_op jit(solution)/shard_map/ppermute | solution.py:16
  174.3 3.2 %copy-start.3 = (s32[2]{0:T(128)}, s32[2]{0:T(128)S(1)}, u32[]{:S(2)}) copy-start(s32[2]{0:T(128)S(1)} %get-tuple-element.10) | copy-start | bytes 28
  275.2 7.8 %copy-start.6 = (pred[2,2]{1,0:T(4,128)(4,1)S(1)}, pred[2,2]{1,0:T(4,128)(4,1)}, u32[]{:S(2)}) copy-start(pred[2,2]{1,0:T(4,128)(4,1)} %compare_and_fusion.2) | copy-start | bytes 16
  275.2 7.8 %copy-start.7 = (pred[2]{0:T(512)(128)(4,1)S(1)}, pred[2]{0:T(512)(128)(4,1)}, u32[]{:S(2)}) copy-start(pred[2]{0:T(512)(128)(4,1)} %compare_and_fusion.1) | copy-start | bytes 10
where the time goes:
time: 296 us; the launch traced here: 295 us
  waiting for transfers between devices  181 us (61%)
  local copies, waits for them, and re-layouts  60.1 us (20%)
  starting transfers between devices  22.2 us (8%)
  other arithmetic  19.1 us (6%)
  matrix products  12.2 us (4%)
    all_to_all x1, waiting for transfers between devices, body(): lax.all_to_all(split, 'ops', split_axis=2, concat_axis=0, tiled=True)  105 us
    all_to_all x1, waiting for transfers between devices, body(): lax.all_to_all(ordered, 'ops', split_axis=0, concat_axis=2, tiled=True)  58.3 us
    ppermute x1, waiting for transfers between devices, with_halo(): lax.ppermute(lax.slice_in_dim(block, block.shape[dim] - width, None, axis...  18.7 us
    gather x1, local copies, waits for them, and re-layouts, body(): ordered = jnp.take(spread, source, axis=0)  15.6 us
    all_to_all x1, starting transfers between devices, body(): lax.all_to_all(split, 'ops', split_axis=2, concat_axis=0, tiled=True)  13.3 us
    dot_general x1, matrix products, body(): jnp.einsum('psba,psbc->psac', targets, half, preferred_element_type=jnp.f...  12.2 us
    gather x2, local copies, waits for them, and re-layouts, body(): targets = jnp.take(kept_near, target_local.reshape(-1), axis=0)  12 us
    unnamed x17, local copies, waits for them, and re-layouts  9.42 us
  transfers between devices with their start and end apart: 4, of which 3 were waited for; matrix products, arithmetic and copies ran while one was open for 10% of the time, Pallas kernels for 0%

commit v1 on v0

--- a/solution.py
+++ b/solution.py
@@ -41,7 +41,9 @@
     offsets = jnp.take(shift, mine)
     strip = width // ops_count
     split = operators.reshape(pair_dev, sector_dev, ops_count, strip, width)
-    spread = lax.all_to_all(split, "ops", split_axis=2, concat_axis=0, tiled=True)
+    shards = jnp.split(split, lax.axis_size("ops"), axis=2)
+    incoming = lax.all_to_all(jnp.stack(shards), "ops", 0, 0)
+    spread = jnp.concatenate(incoming, axis=0)
     ordered = jnp.take(spread, source, axis=0)
     returned = lax.all_to_all(ordered, "ops", split_axis=0, concat_axis=2, tiled=True)
     blocks = returned.reshape(pair_dev, sector_dev, width, width)

time: 296 us -> 361 us (1.22)
  local copies, waits for them, and re-layouts: 60.1 us -> 124 us
    unnamed x17 -> x82, local copies, waits for them, and re-layouts: 9.42 us -> 80.7 us
    reshape x1 -> x0, local copies, waits for them, and re-layouts: 7.75 us -> none  [body(): split = operators.reshape(pair_dev, sector_dev, ops_count, strip, width)]
  transfers between devices with their start and end apart: 4 -> 4, of which waited for: 3 -> 3; matrix products, arithmetic and copies ran while one was open for 10% -> 8% of each run, Pallas kernels for 0% -> 0%
where the time goes in v1:
time: 361 us; the launch traced here: 359 us
  waiting for transfers between devices  182 us (50%)
  local copies, waits for them, and re-layouts  124 us (34%)
  starting transfers between devices  22.2 us (6%)
  other arithmetic  19.1 us (5%)
  matrix products  12.2 us (3%)
    all_to_all x1, waiting for transfers between devices, body(): incoming = lax.all_to_all(jnp.stack(shards), 'ops', 0, 0)  105 us
    unnamed x82, local copies, waits for them, and re-layouts  80.7 us
    all_to_all x1, waiting for transfers between devices, body(): lax.all_to_all(ordered, 'ops', split_axis=0, concat_axis=2, tiled=True)  58.3 us
    ppermute x1, waiting for transfers between devices, with_halo(): lax.ppermute(lax.slice_in_dim(block, block.shape[dim] - width, None, axis...  18.7 us
    gather x1, local copies, waits for them, and re-layouts, body(): ordered = jnp.take(spread, source, axis=0)  15.6 us
    all_to_all x1, starting transfers between devices, body(): incoming = lax.all_to_all(jnp.stack(shards), 'ops', 0, 0)  13.3 us
    dot_general x1, matrix products, body(): jnp.einsum('psba,psbc->psac', targets, half, preferred_element_type=jnp.f...  12.2 us
    gather x2, local copies, waits for them, and re-layouts, body(): targets = jnp.take(kept_near, target_local.reshape(-1), axis=0)  11.9 us
  transfers between devices with their start and end apart: 4, of which 3 were waited for; matrix products, arithmetic and copies ran while one was open for 8% of the time, Pallas kernels for 0%

profile of v1, /device:TPU:1, one launch (start us, length us, event | category | flops | bytes accessed | tf_op | source)
XLA Modules:
  0.0 359.3 jit_solution(6685287857301843329)
XLA Ops:
  0.0 9.4 %copy.205 = bf16[2,2,768,768]{3,1,2,0:T(2,128)(2,1)} copy(bf16[2,2,768,768]{3,2,1,0:T(8,128)(2,1)} %param.5) | data formatting | bytes 9437184 | tf_op args[0]
  9.4 1.7 constant_dynamic-update-slice_fusion.63
  11.1 1.6 constant_dynamic-update-slice_fusion.62
  12.7 1.6 constant_dynamic-update-slice_fusion.61
  14.2 1.6 constant_dynamic-update-slice_fusion.60
  15.8 1.6 constant_dynamic-update-slice_fusion.59
  17.3 1.6 constant_dynamic-update-slice_fusion.58
  18.9 1.6 constant_dynamic-update-slice_fusion.57
  20.5 1.6 constant_dynamic-update-slice_fusion.56
  22.0 1.6 constant_dynamic-update-slice_fusion.55
  23.6 1.6 constant_dynamic-update-slice_fusion.54
  25.2 1.6 constant_dynamic-update-slice_fusion.53
  26.8 1.6 constant_dynamic-update-slice_fusion.52
  28.3 1.6 constant_dynamic-update-slice_fusion.51
  29.9 1.6 constant_dynamic-update-slice_fusion.50
  31.5 1.6 constant_dynamic-update-slice_fusion.49
  33.0 1.6 constant_dynamic-update-slice_fusion.48
  34.6 1.6 constant_dynamic-update-slice_fusion.47
  36.2 1.6 constant_dynamic-update-slice_fusion.46
  37.7 1.6 constant_dynamic-update-slice_fusion.45
  39.3 1.6 constant_dynamic-update-slice_fusion.44
  40.9 1.6 constant_dynamic-update-slice_fusion.43
  42.4 1.6 constant_dynamic-update-slice_fusion.42
  44.0 1.6 constant_dynamic-update-slice_fusion.41
  45.6 1.6 constant_dynamic-update-slice_fusion.40
  47.1 1.6 constant_dynamic-update-slice_fusion.39
  48.7 1.6 constant_dynamic-update-slice_fusion.38
  50.2 1.5 constant_dynamic-update-slice_fusion.37
  51.8 1.6 constant_dynamic-update-slice_fusion.36
  53.4 1.6 constant_dynamic-update-slice_fusion.35
  54.9 1.6 constant_dynamic-update-slice_fusion.34
  56.5 1.6 constant_dynamic-update-slice_fusion.33
  58.0 1.6 constant_dynamic-update-slice_fusion.32
  81.4 13.3 %all-to-all-start = ((bf16[64,2,2,1,12,768]{5,2,4,1,3,0:T(2,128)(2,1)}), bf16[64,2,2,1,12,768]{5,2,4,1,3,0:T(2,128)(2,1)}, u32[]{:S(2)}, u32[]{:S(2)}) async-start(bf16[64,2,2,1,12,768]{5,2,4,1,3,0:T(2,128)(2,1)} %constant_dynamic-update-slice_fusion), calls=%async_computation | async-start | bytes 9437184 | tf_op jit(solution)/shard_map/all_to_all | solution.py:45
  94.7 2.5 sort.17
  97.3 104.5 %all-to-all-done = bf16[64,2,2,1,12,768]{5,2,4,1,3,0:T(2,128)(2,1)} async-done(((bf16[64,2,2,1,12,768]{5,2,4,1,3,0:T(2,128)(2,1)}), bf16[64,2,2,1,12,768]{5,2,4,1,3,0:T(2,128)(2,1)}, u32[]{:S(2)}, u32[]{:S(2)}) %all-to-all-start) | async-done | bytes 4718624 | tf_op jit(solution)/shard_map/all_to_all | solution.py:45
  201.8 15.6 %gather_fusion.4 = bf16[128,2,12,768]{3,1,2,0:T(2,128)(2,1)} fusion(bf16[128,2,12,768]{3,1,2,0:T(2,128)(2,1)} %bitcast.70, s32[1024]{0:T(1024)S(1)} %pad_clamp_fusion), kind=kCustom, calls=%fused_computation.4 | custom fusion | bytes 9437696 | tf_op jit(solution)/shard_map/jit(_take)/gather | solution.py:47
  217.4 8.8 %broadcast_select_fusion = bf16[128,2,1,12,768]{4,1,3,2,0:T(2,128)(2,1)} fusion(pred[128]{0:T(512)(128)(4,1)S(1)} %compare_and_fusion, bf16[128,2,12,768]{3,1,2,0:T(2,128)(2,1)} %gather_fusion.4), kind=kLoop, calls=%fused_computation.5 | loop fusion | flops 2359296 | bytes 9437312 | tf_op jit(solution)/shard_map/jit(_take)/select_n | solution.py:47
  226.2 6.1 %all-to-all-start.1 = ((bf16[128,2,1,12,768]{4,1,3,2,0:T(2,128)(2,1)}), bf16[128,2,1,12,768]{4,1,3,2,0:T(2,128)(2,1)}, u32[]{:S(2)}, u32[]{:S(2)}) async-start(bf16[128,2,1,12,768]{4,1,3,2,0:T(2,128)(2,1)} %broadcast_select_fusion), calls=%async_computation.1 | async-start | bytes 9437184 | tf_op jit(solution)/shard_map/all_to_all | solution.py:48
  232.3 1.6 fusion.32
  243.7 18.7 %collective-permute-done = bf16[1,768,768]{2,1,0:T(8,128)(2,1)S(1)} collective-permute-done((bf16[1,768,768]{2,1,0:T(8,128)(2,1)}, bf16[1,768,768]{2,1,0:T(8,128)(2,1)S(1)}, u32[]{:S(2)}, u32[]{:S(2)}) %collective-permute-start) | collective-permute-done | bytes 1179680 | tf_op jit(solution)/shard_map/ppermute | solution.py:13
  262.5 3.7 %maximum_select_fusion = bf16[4,768,768]{2,1,0:T(8,128)(2,1)} fusion(bf16[1,768,768]{2,1,0:T(8,128)(2,1)} %collective-permute-done.1, bf16[2,768,768]{2,1,0:T(8,128)(2,1)S(1)} %copy-done.3, bf16[1,768,768]{2,1,0:T(8,128)(2,1)S(1)} %collective-permute-done, pred[4,768]{1,0:T(4,128)(4,1)S(1)} %iota_compare_fusion), kind=kLoop, calls=%fused_computation.6 | loop fusion | flops 7077888 | bytes 9440256 | tf_op jit(solution)/shard_map/jit(_where)/select_n | solution.py:37
  266.1 5.3 %gather_fusion.2 = bf16[4,768,768]{2,1,0:T(8,128)(2,1)} fusion(bf16[4,768,768]{2,1,0:T(8,128)(2,1)} %maximum_select_fusion, s32[1024]{0:T(1024)S(1)} %pad_clamp_fusion.2), kind=kCustom, calls=%fused_computation.2 | custom fusion | bytes 9437200 | tf_op jit(solution)/shard_map/jit(_take)/gather | solution.py:54
  271.4 6.6 %copy.204 = bf16[2,2,768,768]{2,3,1,0:T(8,128)(2,1)} copy(bf16[2,2,768,768]{3,2,1,0:T(8,128)(2,1)} %bitcast.406) | data formatting | bytes 9437184 | tf_op jit(solution)/shard_map/jit(_take)/gather | solution.py:54
  278.1 3.0 gather_fusion.3
  281.1 58.3 %all-to-all-done.1 = bf16[128,2,1,12,768]{4,1,3,2,0:T(2,128)(2,1)} async-done(((bf16[128,2,1,12,768]{4,1,3,2,0:T(2,128)(2,1)}), bf16[128,2,1,12,768]{4,1,3,2,0:T(2,128)(2,1)}, u32[]{:S(2)}, u32[]{:S(2)}) %all-to-all-start.1) | async-done | bytes 4718624 | tf_op jit(solution)/shard_map/all_to_all | solution.py:48
  339.4 7.7 %copy.269 = bf16[2,2,64,1,12,768]{5,1,4,2,0,3:T(2,128)(2,1)} copy(bf16[2,2,64,1,12,768]{5,1,4,0,2,3:T(2,128)(2,1)} %bitcast.73) | data formatting | bytes 9437184 | tf_op jit(solution)/shard_map/all_to_all | solution.py:48
  347.2 12.2 %fusion.7 = bf16[2,2,768,768]{3,2,1,0:T(8,128)(2,1)} fusion(bf16[2,2,768,768]{2,3,1,0:T(8,128)(2,1)} %copy.204, pred[2,2]{1,0:T(4,128)(4,1)S(1)} %copy-done.7, bf16[2,2,768,768]{3,1,2,0:T(2,128)(2,1)} %bitcast.471, bf16[2,768,768]{2,1,0:T(8,128)(2,1)S(1)} %gather_fusion.3, pred[2]{0:T(512)(128)(4,1)S(1)} %copy-done.8), kind=kOutput, calls=%fused_computation.14 | convolution fusion | flops 7256014848 | bytes 16515078 | tf_op jit(solution)/shard_map/psba,psbc->psac/dot_general | solution.py:56
  (74 shorter events, 31.6 us)
Async XLA Ops:
  0.0 239.3 %copy-start = (s32[8]{0:T(128)S(1)}, s32[8]{0:T(128)}, u32[]{:S(2)}) copy-start(s32[8]{0:T(128)} %param.9) | copy-start | bytes 100
  9.4 50.2 %copy-start.2 = (bf16[2,2,768,768]{3,1,2,0:T(2,128)(2,1)S(1)}, bf16[2,2,768,768]{3,1,2,0:T(2,128)(2,1)}, u32[]{:S(2)}) copy-start(bf16[2,2,768,768]{3,1,2,0:T(2,128)(2,1)} %copy.205) | copy-start | bytes 14155780
  81.4 13.3 %copy-start.6 = (s32[128]{0:T(128)S(1)}, s32[128]{0:T(128)}, u32[]{:S(2)}) copy-start(s32[128]{0:T(128)} %param.8) | copy-start | bytes 1540
  81.4 120.4 %all-to-all-start = ((bf16[64,2,2,1,12,768]{5,2,4,1,3,0:T(2,128)(2,1)}), bf16[64,2,2,1,12,768]{5,2,4,1,3,0:T(2,128)(2,1)}, u32[]{:S(2)}, u32[]{:S(2)}) async-start(bf16[64,2,2,1,12,768]{5,2,4,1,3,0:T(2,128)(2,1)} %constant_dynamic-update-slice_fusion), calls=%async_computation | async-start | bytes 9437184 | tf_op jit(solution)/shard_map/all_to_all | solution.py:45
  97.2 139.4 %copy-start.5 = (s32[128]{0:T(128)}, s32[128]{0:T(128)S(1)}, u32[]{:S(2)}) copy-start(s32[128]{0:T(128)S(1)} %get-tuple-element.6) | copy-start | bytes 1540
  226.2 6.1 %copy-start.3 = (bf16[2,768,768]{2,1,0:T(8,128)(2,1)S(1)}, bf16[2,768,768]{2,1,0:T(8,128)(2,1)}, u32[]{:S(2)}) copy-start(bf16[2,768,768]{2,1,0:T(8,128)(2,1)} %param.6) | copy-start | bytes 7077892
  226.2 113.3 %all-to-all-start.1 = ((bf16[128,2,1,12,768]{4,1,3,2,0:T(2,128)(2,1)}), bf16[128,2,1,12,768]{4,1,3,2,0:T(2,128)(2,1)}, u32[]{:S(2)}, u32[]{:S(2)}) async-start(bf16[128,2,1,12,768]{4,1,3,2,0:T(2,128)(2,1)} %broadcast_select_fusion), calls=%async_computation.1 | async-start | bytes 9437184 | tf_op jit(solution)/shard_map/all_to_all | solution.py:48
  232.3 4.4 %copy-start.1 = (s32[128]{0:T(128)S(1)}, s32[128]{0:T(128)}, u32[]{:S(2)}) copy-start(s32[128]{0:T(128)} %param.7) | copy-start | bytes 1540
  233.9 28.6 %collective-permute-start = (bf16[1,768,768]{2,1,0:T(8,128)(2,1)}, bf16[1,768,768]{2,1,0:T(8,128)(2,1)S(1)}, u32[]{:S(2)}, u32[]{:S(2)}) collective-permute-start(bf16[1,768,768]{2,1,0:T(8,128)(2,1)} %get-tuple-element.7), channel_id=1, source_target_pairs={{0,1},{1,2},{2,3},{3,0},{4,5},{5,6},{6,7},{7,4},{8,9},{9,10},{10,1... | collective-permute-start | bytes 3538952 | tf_op jit(solution)/shard_map/ppermute | solution.py:13
  235.2 27.3 %collective-permute-start.1 = (bf16[1,768,768]{2,1,0:T(8,128)(2,1)}, bf16[1,768,768]{2,1,0:T(8,128)(2,1)}, u32[]{:S(2)}, u32[]{:S(2)}) collective-permute-start(bf16[1,768,768]{2,1,0:T(8,128)(2,1)} %get-tuple-element.8), channel_id=1, source_target_pairs={{1,0},{2,1},{3,2},{0,3},{5,4},{6,5},{7,6},{4,7},{9,8},{10,9},{11,1... | collective-permute-start | bytes 3538952 | tf_op jit(solution)/shard_map/ppermute | solution.py:16
  238.6 3.1 copy-start.4
  339.4 7.8 %copy-start.7 = (pred[2,2]{1,0:T(4,128)(4,1)S(1)}, pred[2,2]{1,0:T(4,128)(4,1)}, u32[]{:S(2)}) copy-start(pred[2,2]{1,0:T(4,128)(4,1)} %compare_and_fusion.2) | copy-start | bytes 16
  339.4 7.8 %copy-start.8 = (pred[2]{0:T(512)(128)(4,1)S(1)}, pred[2]{0:T(512)(128)(4,1)}, u32[]{:S(2)}) copy-start(pred[2]{0:T(512)(128)(4,1)} %compare_and_fusion.1) | copy-start | bytes 10
